TPU v7x, 32 devices: a whole 2x2x4 slice. The times are simulated.
32 devices in a mesh: pipe: 4 (over x, core), vocab: 8 (over z, y).
Axes of the slice: x: 2, y: 2, z: 4, core: 2. Of those that a mesh axis runs over, the one named last changes fastest.
Arguments:
- hidden: bfloat16 [4, 128, 4096], P('pipe'), may hold values from -60 to 60
- norm_gain: float32 [4096], replicated, may hold values from 0.5 to 1.5
- out_weight: bfloat16 [128256, 4096], P(('pipe', 'vocab')), may hold values from -4 to 4
- targets: int32 [4, 128], P('pipe'), may hold values from 0 to 128255
- loss_mask: int32 [4, 128], P('pipe'), may hold values from 0 to 1, as said below
- slot_position: int32 [4, 128], P('pipe'), may hold values from 0 to 127, each once within a row
- counts: int32 [4], replicated, may hold values from 1 to 128, 320 in all
- loss_scale: float32 [], replicated, may hold values from 4096 to 32768
Outputs:
- loss: float32 [], replicated
- grad_hidden: bfloat16 [4, 128, 4096], P('pipe')
Inputs may be any that keep to these rules, and one draw needn't show every extreme that they name: The 4 counts sum to exactly 320, and one of them equals 128. Each row of slot_position holds every number of 0 to 127 once. Each row of loss_mask holds at least 64 ones.
All inputs are finite; a program needn't handle non-finite values.
Results may differ from a plain program's by a relative error of at most 0.0034.
Values may be sent and summed in bfloat16 or wider, within the bound.
A program may use at most 128 MiB of HBM per device.

v0:
```python
import jax
import jax.numpy as jnp
from jax import lax
from jax.sharding import PartitionSpec as P

EPSILON = 1e-05


def rms_scale(values, norm_gain):
    mean_square = jnp.mean(values * values, axis=-1, keepdims=True)
    return values * lax.rsqrt(mean_square + EPSILON) * norm_gain


def pull_rows(rows, norm_gain, cotangent):
    pullback = jax.vjp(lambda values: rms_scale(values, norm_gain), rows)[1]
    return pullback(cotangent)[0].astype(jnp.bfloat16)


def softmax_stats(logits, local_target):
    row_top = lax.pmax(jnp.max(logits, axis=1), ("pipe", "vocab"))
    local_total = jnp.sum(jnp.exp(logits - row_top[:, None]), axis=1)
    exp_total, target_logit = lax.psum((local_total, local_target), ("pipe", "vocab"))
    return (row_top + jnp.log(exp_total), target_logit)


def body(hidden, norm_gain, out_weight, targets, loss_mask, slot_position, counts, loss_scale):
    micro_slots = hidden.shape[1]
    model_width = hidden.shape[2]
    shard_words = out_weight.shape[0]
    offset = lax.axis_index(("pipe", "vocab")) * shard_words
    own_rows = hidden.reshape(micro_slots, model_width).astype(jnp.float32)
    own_normed = rms_scale(own_rows, norm_gain).astype(jnp.bfloat16)
    all_normed, all_targets, all_masks, all_positions = (
        lax.all_gather(own_normed, "pipe", axis=0, tiled=True),
        lax.all_gather(targets.reshape(micro_slots), "pipe", axis=0, tiled=True),
        lax.all_gather(loss_mask.reshape(micro_slots), "pipe", axis=0, tiled=True),
        lax.all_gather(slot_position.reshape(micro_slots), "pipe", axis=0, tiled=True),
    )
    rows_total = all_normed.shape[0]
    micro_index = jnp.arange(rows_total, dtype=jnp.int32) // micro_slots
    count_row = jnp.sum(
        jnp.where(
            micro_index[:, None] == jnp.arange(counts.shape[0], dtype=jnp.int32)[None, :],
            counts[None, :],
            0,
        ),
        axis=1,
    )
    inside = all_positions < count_row
    token_weight = jnp.where(inside & (all_masks == 1), 1.0, 0.0).astype(jnp.float32)
    weight_total = jnp.sum(token_weight)
    work_normed, work_targets, work_weight = (all_normed, all_targets, token_weight)
    logits = lax.dot_general(
        work_normed, out_weight, (((1,), (1,)), ((), ())), preferred_element_type=jnp.float32
    )
    is_target = (
        jnp.arange(shard_words, dtype=jnp.int32)[None, :] == (work_targets - offset)[:, None]
    )
    local_target = jnp.sum(jnp.where(is_target, logits, 0.0), axis=1)
    log_total, target_logit = softmax_stats(logits, local_target)
    loss = jnp.sum(work_weight * (log_total - target_logit)) / weight_total
    token_coef = loss_scale * work_weight / weight_total
    logit_grad = (
        (jnp.exp(logits - log_total[:, None]) - is_target.astype(jnp.float32)) * token_coef[:, None]
    ).astype(jnp.bfloat16)
    work_grad = jnp.dot(logit_grad, out_weight, preferred_element_type=jnp.float32)
    grad_cube = work_grad.reshape(rows_total // micro_slots, micro_slots, model_width)
    micro_grad = lax.psum_scatter(grad_cube, "pipe", scatter_dimension=0, tiled=True)
    summed = lax.psum(micro_grad, "vocab")
    grad_out = pull_rows(own_rows, norm_gain, summed.reshape(micro_slots, model_width))
    return (loss, grad_out.reshape(1, micro_slots, model_width))


def solution(mesh):
    in_specs = (
        P("pipe", None, None),
        P(),
        P(("pipe", "vocab"), None),
        P("pipe", None),
        P("pipe", None),
        P("pipe", None),
        P(),
        P(),
    )
    out_specs = (P(), P("pipe", None, None))
    return jax.shard_map(body, mesh=mesh, in_specs=in_specs, out_specs=out_specs, check_vma=False)
```

profile of v0, /device:TPU:0, one launch (start us, length us, event | category | flops | bytes accessed | tf_op | source)
XLA Modules:
  0.0 372.7 jit_solution(8846889576664135234)
XLA Ops:
  7.2 0.0 copy-start.3
  7.2 0.0 copy-start.4
  7.2 0.0 copy-start.5
  7.2 0.0 copy-start.6
  7.2 0.0 all-gather.5.cloned.1.call-start
  7.3 1.5 fusion.7
  8.8 2.5 fusion.9
  11.3 0.0 all-gather.5.cloned.1.call-update
  11.3 0.0 reduce-scatter.2.cloned.1.call-start
  12.0 0.0 copy-done.3
  12.0 6.0 %all-gather.2 = s32[1,512]{1,0:T(1,128)S(1)} all-gather(s32[1,128]{1,0:T(1,128)S(1)} %copy-done.3), channel_id=4, replica_groups=mesh['pipe'=4,'vocab'=8] {'pipe'}, dimensions={1}, use_global_device_ids=true | all-gather | bytes 2560 | tf_op jit(solution)/shard_map/all_gather | solution.py:35
  18.1 0.0 copy-done.4
  18.1 5.4 %all-gather.1 = s32[1,512]{1,0:T(1,128)S(1)} all-gather(s32[1,128]{1,0:T(1,128)S(1)} %copy-done.4), channel_id=3, replica_groups=mesh['pipe'=4,'vocab'=8] {'pipe'}, dimensions={1}, use_global_device_ids=true | all-gather | bytes 2560 | tf_op jit(solution)/shard_map/all_gather | solution.py:36
  23.4 0.0 copy-done.5
  23.4 5.2 %all-gather = s32[1,512]{1,0:T(1,128)S(1)} all-gather(s32[1,128]{1,0:T(1,128)S(1)} %copy-done.5), channel_id=2, replica_groups=mesh['pipe'=4,'vocab'=8] {'pipe'}, dimensions={1}, use_global_device_ids=true | all-gather | bytes 2560 | tf_op jit(solution)/shard_map/all_gather | solution.py:37
  28.6 0.0 copy-done.6
  28.6 0.1 select_reduce_fusion.1
  28.7 19.9 %all-gather.5.cloned.1.call-done = bf16[512,4096]{1,0:T(8,128)(2,1)} async-done(((bf16[128,4096]{1,0:T(8,128)(2,1)}), bf16[512,4096]{1,0:T(8,128)(2,1)}) %all-gather.5.cloned.1.call-update) | async-done | bytes 4194320 | tf_op jit(solution)/shard_map/all_gather | solution.py:34
  48.7 23.8 %fusion.18 = (f32[512]{0:T(512)S(1)}, f32[512,4008]{0,1:T(8,128)}) fusion(bf16[512,4096]{1,0:T(8,128)(2,1)} %all-gather.5.cloned.1.call-done, bf16[4008,4096]{1,0:T(8,128)(2,1)} %param.10), kind=kOutput, calls=%fused_computation.41 | convolution fusion | flops 16812822528 | bytes 45238272 | tf_op jit(solution)/shard_map/dot_general | solution.py:53
  72.4 39.2 %pmax.7 = f32[512]{0:T(512)S(1)} all-reduce(f32[512]{0:T(512)S(1)} %get-tuple-element.10), channel_id=1, replica_groups=mesh['pipe'=4,'vocab'=8] {'pipe','vocab'}, use_global_device_ids=true, to_apply=%region_3.4 | all-reduce | flops 512 | bytes 4096 | tf_op jit(solution)/shard_map/pmax | solution.py:20
  111.7 4.5 %select_reduce_fusion = (f32[512]{0:T(512)S(1)}, f32[512]{0:T(512)S(1)}) fusion(f32[512,4008]{0,1:T(8,128)} %get-tuple-element.11, s32[512]{0:T(512)S(1)} %bitcast.27, f32[512]{0:T(512)S(1)} %pmax.7), kind=kLoop, calls=%fused_computation.1 | loop fusion | flops 10259456 | bytes 8216576 | tf_op jit(solution)/shard_map/reduce_sum | solution.py:59
  116.2 41.0 %all-reduce = (f32[512]{0:T(512)S(1)}, f32[512]{0:T(512)S(1)}) all-reduce(f32[512]{0:T(512)S(1)} %get-tuple-element.3, f32[512]{0:T(512)S(1)} %get-tuple-element.2), channel_id=1, replica_groups=mesh['pipe'=4,'vocab'=8] {'pipe','vocab'}, use_global_device_ids=true, to_apply=%region_5.6 | all-reduce | flops 1024 | bytes 8192 | tf_op jit(solution)/shard_map/psum | solution.py:22
  157.1 0.6 select_reduce_fusion.2
  157.8 0.7 fusion.13
  158.4 25.5 %fusion = f32[512,4096]{1,0:T(8,128)} fusion(bf16[4008,4096]{1,0:T(8,128)(2,1)} %param.10, f32[512,4008]{0,1:T(8,128)} %get-tuple-element.11, f32[512]{0:T(512)S(1)} %fusion.13, f32[512]{0:T(512)S(1)} %get-tuple-element.8, s32[512]{0:T(512)S(1)} %bitcast.28), kind=kOutput, calls=%fused_computation.4 | convolution fusion | flops 16823083008 | bytes 49436672 | tf_op jit(solution)/shard_map/dot_general | solution.py:66
  183.9 0.0 copy-start
  183.9 0.0 copy-start.2
  183.9 0.0 reduce-scatter.2.cloned.1.call-update
  184.0 0.0 all-reduce.3.cloned.1.call-start
  184.0 71.2 %reduce-scatter.2.cloned.1.call-done = f32[1,128,4096]{2,1,0:T(8,128)} async-done(((f32[4,128,4096]{2,1,0:T(8,128)}), f32[1,128,4096]{2,1,0:T(8,128)}) %reduce-scatter.2.cloned.1.call-update) | async-done | bytes 2097168 | tf_op jit(solution)/shard_map/reduce_scatter | solution.py:68
  255.3 0.0 all-reduce.3.cloned.1.call-update
  256.6 104.7 %all-reduce.3.cloned.1.call-done = f32[1,128,4096]{2,1,0:T(8,128)} async-done(((f32[1,128,4096]{2,1,0:T(8,128)}), f32[1,128,4096]{2,1,0:T(8,128)}) %all-reduce.3.cloned.1.call-update) | async-done | bytes 2097168 | tf_op jit(solution)/shard_map/psum | solution.py:69
  361.3 0.0 copy-done
  361.3 0.0 copy-done.2
  361.3 0.0 copy-start.1
  361.3 2.1 fusion.10
  363.4 0.1 copy-done.1
  363.5 1.5 fusion.11
  (5 shorter events, 0.0 us)
Async XLA Ops:
  7.2 4.9 %copy-start.3 = (s32[1,128]{1,0:T(1,128)S(1)}, s32[1,128]{1,0:T(1,128)}, u32[]{:S(2)}) copy-start(s32[1,128]{1,0:T(1,128)} %param.11) | copy-start | bytes 1540
  7.2 10.9 %copy-start.4 = (s32[1,128]{1,0:T(1,128)S(1)}, s32[1,128]{1,0:T(1,128)}, u32[]{:S(2)}) copy-start(s32[1,128]{1,0:T(1,128)} %param.12) | copy-start | bytes 1540
  7.2 16.2 %copy-start.5 = (s32[1,128]{1,0:T(1,128)S(1)}, s32[1,128]{1,0:T(1,128)}, u32[]{:S(2)}) copy-start(s32[1,128]{1,0:T(1,128)} %param.13) | copy-start | bytes 1540
  7.2 21.4 %copy-start.6 = (s32[4]{0:T(128)S(1)}, s32[4]{0:T(128)}, u32[]{:S(2)}) copy-start(s32[4]{0:T(128)} %param.14) | copy-start | bytes 52
  7.2 41.5 %all-gather.5.cloned.1.call-start = ((), (), s32[]{:S(2)}) async-start(), calls=%async_computation.1 | async-start | bytes 5242880 | tf_op jit(solution)/shard_map/all_gather | solution.py:34
  11.3 243.9 %reduce-scatter.2.cloned.1.call-start = ((), (), s32[]{:S(2)}) async-start(), calls=%async_computation.2 | async-start | bytes 10485760 | tf_op jit(solution)/shard_map/reduce_scatter | solution.py:68
  183.9 177.3 %copy-start = (bf16[1,128,4096]{2,1,0:T(8,128)(2,1)S(1)}, bf16[1,128,4096]{2,1,0:T(8,128)(2,1)}, u32[]{:S(2)}) copy-start(bf16[1,128,4096]{2,1,0:T(8,128)(2,1)} %param.8) | copy-start | bytes 3145732
  183.9 177.3 %copy-start.2 = (f32[4096]{0:T(1024)S(1)}, f32[4096]{0:T(1024)}, u32[]{:S(2)}) copy-start(f32[4096]{0:T(1024)} %param.9) | copy-start | bytes 49156
  184.0 177.3 %all-reduce.3.cloned.1.call-start = ((), (), s32[]{:S(2)}) async-start(), calls=%async_computation.3 | async-start | bytes 4194304 | tf_op jit(solution)/shard_map/psum | solution.py:69
  361.3 2.2 copy-start.1
Sparse Core Ops, SparseCore 0:
  11.5 37.1 all-gather.4
  184.1 71.1 reduce-scatter.1
  258.9 102.3 all-reduce.2
where the time goes:
time: 373 us
  waiting for transfers between devices  196 us (53%)
  blocking collectives  96.8 us (26%)
  matrix products  49.3 us (13%)
  between operations  16.9 us (5%)
  other arithmetic  13.6 us (4%)
    psum x1, waiting for transfers between devices, body(): summed = lax.psum(micro_grad, 'vocab')  105 us
    reduce_scatter x1, waiting for transfers between devices, body(): lax.psum_scatter(grad_cube, 'pipe', scatter_dimension=0, tiled=True)  71.2 us
    psum x1, blocking collectives, softmax_stats(): lax.psum((local_total, local_target), ('pipe', 'vocab'))  41 us
    pmax x1, blocking collectives, softmax_stats(): row_top = lax.pmax(jnp.max(logits, axis=1), ('pipe', 'vocab'))  39.2 us
    dot_general x1, matrix products, body(): jnp.dot(logit_grad, out_weight, preferred_element_type=jnp.float32)  25.5 us
    dot_general x1, matrix products, body(): lax.dot_general(work_normed, out_weight, (((1,), (1,)), ((), ())), prefer...  23.8 us
    all_gather x1, waiting for transfers between devices, body(): lax.all_gather(own_normed, 'pipe', axis=0, tiled=True)  19.9 us
  transfers between devices with their start and end apart: 3, of which 3 were waited for; matrix products, arithmetic and copies ran while one was open for 0% of the time, Pallas kernels for 0%

commit v1 on v0

--- a/solution.py
+++ b/solution.py
@@ -66,7 +66,7 @@
     work_grad = jnp.dot(logit_grad, out_weight, preferred_element_type=jnp.float32)
     grad_cube = work_grad.reshape(rows_total // micro_slots, micro_slots, model_width)
     micro_grad = lax.psum_scatter(grad_cube, "pipe", scatter_dimension=0, tiled=True)
-    summed = lax.psum(micro_grad, "vocab")
+    summed = jnp.sum(lax.all_gather(micro_grad, "vocab"), axis=0)
     grad_out = pull_rows(own_rows, norm_gain, summed.reshape(micro_slots, model_width))
     return (loss, grad_out.reshape(1, micro_slots, model_width))
 

time: 373 us -> 502 us (1.35)
  waiting for transfers between devices: 196 us -> 319 us
  other arithmetic: 13.6 us -> 19.2 us
    all_gather x0 -> x1, waiting for transfers between devices: none -> 228 us  [body(): summed = jnp.sum(lax.all_gather(micro_grad, 'vocab'), axis=0)]
    psum x1 -> x0, waiting for transfers between devices: 105 us -> none  [body(): summed = lax.psum(micro_grad, 'vocab')]
    reduce_sum x0 -> x1, other arithmetic: none -> 7.43 us  [body(): summed = jnp.sum(lax.all_gather(micro_grad, 'vocab'), axis=0)]
where the time goes in v1:
time: 502 us
  waiting for transfers between devices  319 us (64%)
  blocking collectives  96.7 us (19%)
  matrix products  49.3 us (10%)
  other arithmetic  19.2 us (4%)
  between operations  17 us (3%)
    all_gather x1, waiting for transfers between devices, body(): summed = jnp.sum(lax.all_gather(micro_grad, 'vocab'), axis=0)  228 us
    reduce_scatter x1, waiting for transfers between devices, body(): lax.psum_scatter(grad_cube, 'pipe', scatter_dimension=0, tiled=True)  71.1 us
    psum x1, blocking collectives, softmax_stats(): lax.psum((local_total, local_target), ('pipe', 'vocab'))  40.9 us
    pmax x1, blocking collectives, softmax_stats(): row_top = lax.pmax(jnp.max(logits, axis=1), ('pipe', 'vocab'))  39.2 us
    dot_general x1, matrix products, body(): jnp.dot(logit_grad, out_weight, preferred_element_type=jnp.float32)  25.5 us
    dot_general x1, matrix products, body(): lax.dot_general(work_normed, out_weight, (((1,), (1,)), ((), ())), prefer...  23.7 us
    all_gather x1, waiting for transfers between devices, body(): lax.all_gather(own_normed, 'pipe', axis=0, tiled=True)  19.9 us
  transfers between devices with their start and end apart: 3, of which 3 were waited for; matrix products, arithmetic and copies ran while one was open for 0% of the time, Pallas kernels for 0%

profile of v1, /device:TPU:0, one launch (start us, length us, event | category | flops | bytes accessed | tf_op | source)
XLA Modules:
  0.0 501.7 jit_solution(14745181805273271279)
XLA Ops:
  7.2 0.0 copy-start.2
  7.2 0.0 copy-start.3
  7.2 0.0 copy-start.4
  7.2 0.0 copy-start.5
  7.2 0.0 all-gather.7.cloned.1.call-start
  7.3 1.5 fusion.7
  8.8 2.5 fusion.9
  11.3 0.0 all-gather.7.cloned.1.call-update
  11.3 0.0 reduce-scatter.2.cloned.1.call-start
  12.0 0.0 copy-done.2
  12.0 6.0 %all-gather.2 = s32[1,512]{1,0:T(1,128)S(1)} all-gather(s32[1,128]{1,0:T(1,128)S(1)} %copy-done.2), channel_id=4, replica_groups=mesh['pipe'=4,'vocab'=8] {'pipe'}, dimensions={1}, use_global_device_ids=true | all-gather | bytes 2560 | tf_op jit(solution)/shard_map/all_gather | solution.py:35
  18.1 0.0 copy-done.3
  18.1 5.4 %all-gather.1 = s32[1,512]{1,0:T(1,128)S(1)} all-gather(s32[1,128]{1,0:T(1,128)S(1)} %copy-done.3), channel_id=3, replica_groups=mesh['pipe'=4,'vocab'=8] {'pipe'}, dimensions={1}, use_global_device_ids=true | all-gather | bytes 2560 | tf_op jit(solution)/shard_map/all_gather | solution.py:36
  23.4 0.0 copy-done.4
  23.4 5.2 %all-gather = s32[1,512]{1,0:T(1,128)S(1)} all-gather(s32[1,128]{1,0:T(1,128)S(1)} %copy-done.4), channel_id=2, replica_groups=mesh['pipe'=4,'vocab'=8] {'pipe'}, dimensions={1}, use_global_device_ids=true | all-gather | bytes 2560 | tf_op jit(solution)/shard_map/all_gather | solution.py:37
  28.6 0.0 copy-done.5
  28.6 0.1 select_reduce_fusion.1
  28.7 19.9 %all-gather.7.cloned.1.call-done = bf16[512,4096]{1,0:T(8,128)(2,1)} async-done(((bf16[128,4096]{1,0:T(8,128)(2,1)}), bf16[512,4096]{1,0:T(8,128)(2,1)}) %all-gather.7.cloned.1.call-update) | async-done | bytes 4194320 | tf_op jit(solution)/shard_map/all_gather | solution.py:34
  48.7 23.7 %fusion.19 = (f32[512]{0:T(512)S(1)}, f32[512,4008]{0,1:T(8,128)}) fusion(bf16[512,4096]{1,0:T(8,128)(2,1)} %all-gather.7.cloned.1.call-done, bf16[4008,4096]{1,0:T(8,128)(2,1)} %param.10), kind=kOutput, calls=%fused_computation.42 | convolution fusion | flops 16812822528 | bytes 45238272 | tf_op jit(solution)/shard_map/dot_general | solution.py:53
  72.4 39.2 %pmax.7 = f32[512]{0:T(512)S(1)} all-reduce(f32[512]{0:T(512)S(1)} %get-tuple-element.10), channel_id=1, replica_groups=mesh['pipe'=4,'vocab'=8] {'pipe','vocab'}, use_global_device_ids=true, to_apply=%region_3.4 | all-reduce | flops 512 | bytes 4096 | tf_op jit(solution)/shard_map/pmax | solution.py:20
  111.7 4.5 select_reduce_fusion
  116.2 40.9 %all-reduce = (f32[512]{0:T(512)S(1)}, f32[512]{0:T(512)S(1)}) all-reduce(f32[512]{0:T(512)S(1)} %get-tuple-element.3, f32[512]{0:T(512)S(1)} %get-tuple-element.2), channel_id=1, replica_groups=mesh['pipe'=4,'vocab'=8] {'pipe','vocab'}, use_global_device_ids=true, to_apply=%region_5.6 | all-reduce | flops 1024 | bytes 8192 | tf_op jit(solution)/shard_map/psum | solution.py:22
  157.1 0.6 select_reduce_fusion.2
  157.7 0.7 fusion.14
  158.4 25.5 %fusion = f32[512,4096]{1,0:T(8,128)} fusion(bf16[4008,4096]{1,0:T(8,128)(2,1)} %param.10, f32[512,4008]{0,1:T(8,128)} %get-tuple-element.11, f32[512]{0:T(512)S(1)} %fusion.14, f32[512]{0:T(512)S(1)} %get-tuple-element.8, s32[512]{0:T(512)S(1)} %bitcast.30), kind=kOutput, calls=%fused_computation.4 | convolution fusion | flops 16823083008 | bytes 49436672 | tf_op jit(solution)/shard_map/dot_general | solution.py:66
  183.9 0.0 reduce-scatter.2.cloned.1.call-update
  183.9 0.2 all-gather.9.cloned.1.call-start
  184.2 71.1 %reduce-scatter.2.cloned.1.call-done = f32[1,128,4096]{2,1,0:T(8,128)} async-done(((f32[4,128,4096]{2,1,0:T(8,128)}), f32[1,128,4096]{2,1,0:T(8,128)}) %reduce-scatter.2.cloned.1.call-update) | async-done | bytes 2097168 | tf_op jit(solution)/shard_map/reduce_scatter | solution.py:68
  255.3 0.0 all-gather.9.cloned.1.call-update
  256.6 0.0 copy-start
  256.6 0.0 copy-start.1
  256.7 228.1 %all-gather.9.cloned.1.call-done = f32[8,128,4096]{2,1,0:T(8,128)} async-done(((f32[1,128,4096]{2,1,0:T(8,128)}), f32[8,128,4096]{2,1,0:T(8,128)}) %all-gather.9.cloned.1.call-update) | async-done | bytes 16777232 | tf_op jit(solution)/shard_map/all_gather | solution.py:69
  484.7 7.4 %reduce.1 = f32[128,4096]{1,0:T(8,128)S(1)} reduce(f32[8,128,4096]{2,1,0:T(8,128)} %all-gather.9.cloned.1.call-done, f32[]{:T(128)} %constant.37.clone.1), dimensions={0}, to_apply=%region_11.12 | reduce | flops 3670016 | bytes 18874372 | tf_op jit(solution)/shard_map/reduce_sum | solution.py:69
  492.2 0.0 copy-done
  492.2 0.0 copy-done.1
  492.2 0.4 fusion.10
  492.6 1.5 fusion.11
  (5 shorter events, 0.0 us)
Async XLA Ops:
  7.2 4.9 copy-start.2
  7.2 10.9 %copy-start.3 = (s32[1,128]{1,0:T(1,128)S(1)}, s32[1,128]{1,0:T(1,128)}, u32[]{:S(2)}) copy-start(s32[1,128]{1,0:T(1,128)} %param.12) | copy-start | bytes 1540
  7.2 16.2 %copy-start.4 = (s32[1,128]{1,0:T(1,128)S(1)}, s32[1,128]{1,0:T(1,128)}, u32[]{:S(2)}) copy-start(s32[1,128]{1,0:T(1,128)} %param.13) | copy-start | bytes 1540
  7.2 21.4 %copy-start.5 = (s32[4]{0:T(128)S(1)}, s32[4]{0:T(128)}, u32[]{:S(2)}) copy-start(s32[4]{0:T(128)} %param.14) | copy-start | bytes 52
  7.2 41.5 %all-gather.7.cloned.1.call-start = ((), (), s32[]{:S(2)}) async-start(), calls=%async_computation.1 | async-start | bytes 5242880 | tf_op jit(solution)/shard_map/all_gather | solution.py:34
  11.3 243.9 %reduce-scatter.2.cloned.1.call-start = ((), (), s32[]{:S(2)}) async-start(), calls=%async_computation.2 | async-start | bytes 10485760 | tf_op jit(solution)/shard_map/reduce_scatter | solution.py:68
  183.9 300.8 %all-gather.9.cloned.1.call-start = ((), (), s32[]{:S(2)}) async-start(), calls=%async_computation.3 | async-start | bytes 18874368 | tf_op jit(solution)/shard_map/all_gather | solution.py:69
  256.6 235.5 %copy-start = (bf16[1,128,4096]{2,1,0:T(8,128)(2,1)S(1)}, bf16[1,128,4096]{2,1,0:T(8,128)(2,1)}, u32[]{:S(2)}) copy-start(bf16[1,128,4096]{2,1,0:T(8,128)(2,1)} %param.8) | copy-start | bytes 3145732
  256.6 235.5 %copy-start.1 = (f32[4096]{0:T(1024)S(1)}, f32[4096]{0:T(1024)}, u32[]{:S(2)}) copy-start(f32[4096]{0:T(1024)} %param.9) | copy-start | bytes 49156
Sparse Core Ops, SparseCore 0:
  11.5 37.1 all-gather.6
  184.0 71.1 reduce-scatter.1
  257.4 227.2 all-gather.8
